TPU v7x, 32 devices: a whole 2x2x4 slice. The times are simulated.
32 devices in a mesh: gx: 4 (over y, core), gy: 4 (over z), gz: 2 (over x).
Axes of the slice: x: 2, y: 2, z: 4, core: 2. Of those that a mesh axis runs over, the one named last changes fastest.
Arguments:
- face_blocks: float32 [4, 4, 2, 6, 16384], P('gx', 'gy', 'gz'), may hold values from -6 to 6
- owner_rank: int32 [4, 4, 2, 6, 1], P('gx', 'gy', 'gz'), may hold values from 0 to 3; in each aligned block of 6 rows (0 to 5, 6 to 11, ..., all dimensions but the last counted through in order) at most 2 rows name the same one
- owner_tile: int32 [4, 4, 2, 6], P('gx', 'gy', 'gz'), may hold values from 0 to 31
- live_count: int32 [4, 4, 2], P('gx', 'gy', 'gz'), may hold values from 1 to 6, as said below
- right_side: float32 [64, 256, 256], P('gx', 'gy', 'gz'), may hold values from -8 to 8
- diagonal: float32 [64, 256, 256], P('gx', 'gy', 'gz'), may hold values from 0.05 to 1
Outputs:
- solution_field: float32 [64, 256, 256], P('gx', 'gy', 'gz')
- residual: float32 [64, 256, 256], P('gx', 'gy', 'gz')
Inputs may be any that keep to these rules, and one draw needn't show every extreme that they name: `owner_rank`: on one device no owner is named by more than 2 of the 6 slots, live or not; some owner is named exactly 2 times on some devices. `live_count`: some device has all 6 slots live in every draw.
All inputs are finite; a program needn't handle non-finite values.
Results may differ from a plain program's by a relative error of at most 0.00012.
Values sent between devices are 32-bit elements; how exact they have to be, the bound alone decides.
A program may use at most 64 MiB of HBM per device.

v0:
```python
import jax
import jax.numpy as jnp
from jax import lax
from jax.sharding import PartitionSpec as P

BLK = 128
CAP = 2
ITERS = 2


def padded_2(cells, sides, width):
    for axis, dim in sides:
        count = lax.axis_size(axis)
        ends = count - 1
        head = lax.slice_in_dim(cells, 0, width, axis=dim)
        tail = lax.slice_in_dim(cells, cells.shape[dim] - width, cells.shape[dim], axis=dim)
        cells = jnp.concatenate(
            [
                lax.ppermute(tail, axis, [(i, (i + 1) % count) for i in range(ends)]),
                cells,
                lax.ppermute(head, axis, [((i + 1) % count, i) for i in range(ends)]),
            ],
            axis=dim,
        )
    return cells


def restrict(values):
    half = BLK // 2
    shaped = values.reshape(values.shape[:-1] + (half, 2, half, 2))
    summed = 0.25 * jnp.sum(shaped, axis=(-3, -1))
    return summed.reshape(values.shape[:-1] + (half * half,))


def operate(field, diagonal):
    padded = padded_2(field, (("gx", 0), ("gy", 1), ("gz", 2)), 1)
    beside = padded[2:, 1:-1, 1:-1] + padded[:-2, 1:-1, 1:-1]
    beside = beside + padded[1:-1, 2:, 1:-1] + padded[1:-1, :-2, 1:-1]
    beside = beside + padded[1:-1, 1:-1, 2:] + padded[1:-1, 1:-1, :-2]
    return (6.0 + diagonal) * field - beside


def paired(residual, image):
    return lax.psum((jnp.sum(residual * residual), jnp.sum(residual * image)), ("gx", "gy", "gz"))


def per_device(face_blocks, owner_rank, owner_tile, live_count, right_side, diagonal):
    block_count = face_blocks.shape[3]
    block_width = face_blocks.shape[4]
    block_rows = face_blocks.reshape(block_count, block_width)
    group_size = lax.axis_size("gx")
    order = jnp.arange(block_count, dtype=jnp.int32)
    living = order < live_count.reshape(())
    target = owner_rank.reshape(block_count)
    before_mask = (
        (target[:, None] == target[None, :]) & (order[None, :] < order[:, None]) & living[None, :]
    )
    position = jnp.sum(before_mask.astype(jnp.int32), axis=1)
    destination_slot = target * CAP + position
    slot_range = jnp.arange(group_size * CAP, dtype=jnp.int32)
    packing = ((destination_slot[None, :] == slot_range[:, None]) & living[None, :]).astype(
        jnp.float32
    )
    tile_labels = (owner_tile.reshape(block_count) + 1).astype(jnp.float32)
    labels = jnp.dot(packing, tile_labels, precision=lax.Precision.HIGHEST).reshape(group_size, CAP)
    packed = jnp.dot(packing, block_rows, precision=lax.Precision.HIGHEST)
    received, received_tags = (
        lax.all_to_all(
            packed.reshape(group_size, CAP, -1), "gx", split_axis=0, concat_axis=0, tiled=True
        ),
        lax.all_to_all(labels, "gx", split_axis=0, concat_axis=0, tiled=True),
    )
    layers = right_side.shape[0]
    incoming = received.reshape(group_size * CAP, -1)
    tag_flat = received_tags.reshape(group_size * CAP)
    tile_range = (jnp.arange(2 * layers, dtype=jnp.int32) + 1).astype(jnp.float32)
    placing = (tag_flat[None, :] == tile_range[:, None]).astype(jnp.float32)
    tile_sums = jnp.dot(placing, incoming, precision=lax.Precision.HIGHEST)
    tile_sums = restrict(tile_sums)
    half = BLK // 2
    source = jnp.transpose(tile_sums.reshape(layers, 2, half, half), (0, 2, 1, 3)).reshape(
        layers, half, 2 * half
    )
    load = right_side + source
    solution_field = jnp.zeros_like(load)
    residual = load
    image = operate(residual, diagonal)
    norm_now, product = paired(residual, image)
    alpha = norm_now / product
    direction, along = (residual, image)
    for iteration in range(ITERS):
        solution_field = solution_field + alpha * direction
        residual = residual - alpha * along
        if iteration + 1 < ITERS:
            image = operate(residual, diagonal)
            norm_next, product = paired(residual, image)
            ratio = norm_next / norm_now
            alpha = norm_next / (product - ratio * norm_next / alpha)
            direction = residual + ratio * direction
            along = image + ratio * along
            norm_now = norm_next
    return (solution_field, residual)


def solution(mesh):
    return jax.shard_map(
        per_device,
        mesh=mesh,
        in_specs=(
            P("gx", "gy", "gz", None, None),
            P("gx", "gy", "gz", None, None),
            P("gx", "gy", "gz", None),
            P("gx", "gy", "gz"),
            P("gx", "gy", "gz"),
            P("gx", "gy", "gz"),
        ),
        out_specs=(P("gx", "gy", "gz"), P("gx", "gy", "gz")),
        check_vma=False,
    )
```

profile of v0, /device:TPU:0, one launch (start us, length us, event | category | flops | bytes accessed | tf_op | source)
XLA Modules:
  0.0 190.4 jit_solution(3773399230261475277)
XLA Ops:
  1.3 0.9 convert_reduce_fusion
  4.5 4.3 %all-to-all-start = ((f32[4,1,2]{2,1,0:T(1,128)}), f32[4,1,2]{2,1,0:T(1,128)S(1)}, u32[]{:S(2)}, u32[]{:S(2)}) async-start(f32[4,1,2]{2,1,0:T(1,128)} %copy.32), calls=%async_computation | async-start | bytes 4096 | tf_op jit(solution)/shard_map/all_to_all | solution.py:71
  8.7 2.7 %fusion.17 = f32[4,2,16384]{2,1,0:T(2,128)} fusion(f32[1,1,1,6,16384]{4,2,3,1,0:T(1,128)} %param.6, pred[4,2,6]{2,0,1:T(4,128)(4,1)S(1)} %compare_and_fusion), kind=kOutput, calls=%fused_computation.53 | convolution fusion | flops 9437184 | bytes 917552 | tf_op jit(solution)/shard_map/dot_general | solution.py:66
  11.4 1.0 all-to-all-done
  12.4 3.5 %all-to-all-start.1 = ((f32[4,2,16384]{2,1,0:T(2,128)}), f32[4,2,16384]{2,1,0:T(2,128)S(1)}, u32[]{:S(2)}, u32[]{:S(2)}) async-start(f32[4,2,16384]{2,1,0:T(2,128)} %fusion.17), calls=%async_computation.1 | async-start | bytes 1048576 | tf_op jit(solution)/shard_map/all_to_all | solution.py:68
  17.2 7.5 %all-to-all-done.1 = f32[4,2,16384]{2,1,0:T(2,128)S(1)} async-done(((f32[4,2,16384]{2,1,0:T(2,128)}), f32[4,2,16384]{2,1,0:T(2,128)S(1)}, u32[]{:S(2)}, u32[]{:S(2)}) %all-to-all-start.1) | async-done | bytes 524320 | tf_op jit(solution)/shard_map/all_to_all | solution.py:68
  25.1 5.3 %copy.34 = f32[16384,8]{1,0:T(8,128)} copy(f32[16384,8]{0,1:T(8,128)S(1)} %bitcast.29) | data formatting | bytes 1048576 | tf_op jit(solution)/shard_map/dot_general | solution.py:78
  30.3 15.2 %fusion.2 = f32[32,64,64]{2,0,1:T(8,128)S(1)} fusion(f32[64,2,64,2,8]{4,3,2,1,0:T(2,128)} %bitcast.27, f32[32]{0:T(128)S(1)} %add_convert_fusion, f32[8]{0:T(128)S(1)} %eq.63), kind=kOutput, calls=%fused_computation.2 | convolution fusion | flops 50725120 | bytes 1048736 | tf_op jit(solution)/shard_map/dot_general | solution.py:78
  46.2 0.8 copy.37
  47.7 1.4 collective-permute-start.1
  49.2 1.3 collective-permute-start
  50.5 2.3 %collective-permute-done = f32[1,64,128]{2,1,0:T(8,128)S(1)} collective-permute-done((f32[1,64,128]{2,1,0:T(8,128)S(1)}, f32[1,64,128]{2,1,0:T(8,128)S(1)}, u32[]{:S(2)}, u32[]{:S(2)}) %collective-permute-start) | collective-permute-done | bytes 32800 | tf_op jit(solution)/shard_map/ppermute | solution.py:21
  52.8 3.9 %collective-permute-start.3 = (f32[18,1,128]{2,1,0:T(1,128)S(1)}, f32[18,1,128]{2,1,0:T(1,128)S(1)}, u32[]{:S(2)}, u32[]{:S(2)}) collective-permute-start(f32[18,1,128]{2,1,0:T(1,128)S(1)} %get-tuple-element.18), channel_id=1, source_target_pairs={{0,2},{2,4},{4,6},{1,3},{3,5},{5,7},{8,10},{10,12},{12,14},{9,11},... | collective-permute-start | bytes 27656 | tf_op jit(solution)/shard_map/ppermute | solution.py:19
  56.7 1.3 collective-permute-start.2
  58.0 4.2 %collective-permute-done.2 = f32[18,1,128]{2,1,0:T(1,128)S(1)} collective-permute-done((f32[18,1,128]{2,1,0:T(1,128)S(1)}, f32[18,1,128]{2,1,0:T(1,128)S(1)}, u32[]{:S(2)}, u32[]{:S(2)}) %collective-permute-start.2) | collective-permute-done | bytes 9248 | tf_op jit(solution)/shard_map/ppermute | solution.py:21
  62.8 1.5 collective-permute-start.4
  64.6 4.5 %collective-permute-start.5 = (f32[18,66,1]{1,2,0:T(1,128)S(1)}, f32[18,66,1]{1,2,0:T(1,128)S(1)}, u32[]{:S(2)}, u32[]{:S(2)}) collective-permute-start(f32[18,66,1]{1,2,0:T(1,128)S(1)} %copy.40), channel_id=1, source_target_pairs={{0,1},{2,3},{4,5},{6,7},{8,9},{10,11},{12,13},{14,15},{16,17},{18,... | collective-permute-start | bytes 14264 | tf_op jit(solution)/shard_map/ppermute | solution.py:19
  69.5 1.0 collective-permute-done.5
  70.8 1.2 multiply_reduce_fusion.2
  72.1 42.5 %all-reduce.1 = (f32[]{:T(128)}, f32[]{:T(128)}) all-reduce(f32[]{:T(128)} %get-tuple-element.5, f32[]{:T(128)} %get-tuple-element.4), channel_id=1, replica_groups=mesh['gx'=4,'gy'=4,'gz'=2] {'gx','gy','gz'}, use_global_device_ids=true, to_apply=%region_3.0 | all-reduce | flops 2 | bytes 16 | tf_op jit(solution)/shard_map/psum | solution.py:44
  115.9 1.3 collective-permute-start.7
  117.2 1.3 collective-permute-start.6
  118.5 4.6 %collective-permute-done.6 = f32[1,64,128]{2,1,0:T(8,128)S(1)} collective-permute-done((f32[1,64,128]{2,1,0:T(8,128)S(1)}, f32[1,64,128]{2,1,0:T(8,128)S(1)}, u32[]{:S(2)}, u32[]{:S(2)}) %collective-permute-start.6) | collective-permute-done | bytes 32800 | tf_op jit(solution)/shard_map/ppermute | solution.py:21
  123.1 2.2 %collective-permute-start.9 = (f32[18,1,128]{2,1,0:T(1,128)S(1)}, f32[18,1,128]{2,1,0:T(1,128)S(1)}, u32[]{:S(2)}, u32[]{:S(2)}) collective-permute-start(f32[18,1,128]{2,1,0:T(1,128)S(1)} %get-tuple-element.16), channel_id=1, source_target_pairs={{0,2},{2,4},{4,6},{1,3},{3,5},{5,7},{8,10},{10,12},{12,14},{9,11},... | collective-permute-start | bytes 27656 | tf_op jit(solution)/shard_map/ppermute | solution.py:19
  125.3 1.3 collective-permute-start.8
  126.6 4.2 %collective-permute-done.8 = f32[18,1,128]{2,1,0:T(1,128)S(1)} collective-permute-done((f32[18,1,128]{2,1,0:T(1,128)S(1)}, f32[18,1,128]{2,1,0:T(1,128)S(1)}, u32[]{:S(2)}, u32[]{:S(2)}) %collective-permute-start.8) | collective-permute-done | bytes 9248 | tf_op jit(solution)/shard_map/ppermute | solution.py:21
  131.4 1.3 collective-permute-start.10
  133.0 4.5 %collective-permute-start.11 = (f32[18,66,1]{1,2,0:T(1,128)S(1)}, f32[18,66,1]{1,2,0:T(1,128)S(1)}, u32[]{:S(2)}, u32[]{:S(2)}) collective-permute-start(f32[18,66,1]{1,2,0:T(1,128)S(1)} %copy.44), channel_id=1, source_target_pairs={{0,1},{2,3},{4,5},{6,7},{8,9},{10,11},{12,13},{14,15},{16,17},{18,... | collective-permute-start | bytes 14264 | tf_op jit(solution)/shard_map/ppermute | solution.py:19
  137.9 1.0 collective-permute-done.11
  139.2 2.1 %multiply_reduce_fusion = (f32[]{:T(128)}, f32[]{:T(128)}, f32[16,64,128]{2,1,0:T(8,128)}) fusion(f32[16,64,128]{2,1,0:T(8,128)S(1)} %multiply_subtract_fusion.1, f32[18,1,128]{2,1,0:T(1,128)S(1)} %collective-permute-done.8, f32[1,64,128]{2,1,0:T(8,128)S(1)} %collective-permute-done.6, f32[1,64,128]{2,1,0:T(8,128)S(1)} %collective-permute-done.7, ...), kind=kLoop, calls=%fused_computation.58 | loop fusion | flops 3932158 | bytes 1666344 | tf_op jit(solution)/shard_map/reduce_sum | solution.py:44
  141.3 42.5 %all-reduce = (f32[]{:T(128)}, f32[]{:T(128)}) all-reduce(f32[]{:T(128)} %get-tuple-element.3, f32[]{:T(128)} %get-tuple-element.2), channel_id=1, replica_groups=mesh['gx'=4,'gy'=4,'gz'=2] {'gx','gy','gz'}, use_global_device_ids=true, to_apply=%region_7.0 | all-reduce | flops 2 | bytes 16 | tf_op jit(solution)/shard_map/psum | solution.py:44
  188.2 2.2 %multiply_subtract_fusion = (f32[16,64,128]{2,1,0:T(8,128)}, f32[16,64,128]{2,1,0:T(8,128)}) fusion(f32[16,64,128]{2,1,0:T(8,128)S(1)} %multiply_subtract_fusion.1, f32[16,64,128]{2,1,0:T(8,128)} %get-tuple-element.10, f32[16,64,128]{2,1,0:T(8,128)S(1)} %get-tuple-element.11, f32[]{:T(128)S(6)} %div.13, f32[]{:T(128)S(6)} %div.15, ...), kind=kLoop, calls=%fused_computation.56 | loop fusion | flops 1179648 | bytes 3145740 | tf_op jit(solution)/shard_map/sub | solution.py:93
  (42 shorter events, 8.5 us)
Async XLA Ops:
  4.5 8.0 %all-to-all-start = ((f32[4,1,2]{2,1,0:T(1,128)}), f32[4,1,2]{2,1,0:T(1,128)S(1)}, u32[]{:S(2)}, u32[]{:S(2)}) async-start(f32[4,1,2]{2,1,0:T(1,128)} %copy.32), calls=%async_computation | async-start | bytes 4096 | tf_op jit(solution)/shard_map/all_to_all | solution.py:71
  12.4 12.3 %all-to-all-start.1 = ((f32[4,2,16384]{2,1,0:T(2,128)}), f32[4,2,16384]{2,1,0:T(2,128)S(1)}, u32[]{:S(2)}, u32[]{:S(2)}) async-start(f32[4,2,16384]{2,1,0:T(2,128)} %fusion.17), calls=%async_computation.1 | async-start | bytes 1048576 | tf_op jit(solution)/shard_map/all_to_all | solution.py:68
  30.3 17.3 %copy-start.1 = (f32[16,64,128]{2,1,0:T(8,128)S(1)}, f32[16,64,128]{2,1,0:T(8,128)}, u32[]{:S(2)}) copy-start(f32[16,64,128]{2,1,0:T(8,128)} %param.10) | copy-start | bytes 1572868
  45.5 25.3 %copy-start = (f32[16,64,128]{2,1,0:T(8,128)S(1)}, f32[16,64,128]{2,1,0:T(8,128)}, u32[]{:S(2)}) copy-start(f32[16,64,128]{2,1,0:T(8,128)} %param.11) | copy-start | bytes 1572868
  47.7 2.8 %collective-permute-start.1 = (f32[1,64,128]{2,1,0:T(8,128)S(1)}, f32[1,64,128]{2,1,0:T(8,128)S(1)}, u32[]{:S(2)}, u32[]{:S(2)}) collective-permute-start(f32[1,64,128]{2,1,0:T(8,128)S(1)} %get-tuple-element.24), channel_id=1, source_target_pairs={{0,8},{8,16},{16,24},{1,9},{9,17},{17,25},{2,10},{10,18},{18,26},{... | collective-permute-start | bytes 98312 | tf_op jit(solution)/shard_map/ppermute | solution.py:19
  49.2 3.6 %collective-permute-start = (f32[1,64,128]{2,1,0:T(8,128)S(1)}, f32[1,64,128]{2,1,0:T(8,128)S(1)}, u32[]{:S(2)}, u32[]{:S(2)}) collective-permute-start(f32[1,64,128]{2,1,0:T(8,128)S(1)} %get-tuple-element.25), channel_id=1, source_target_pairs={{8,0},{16,8},{24,16},{9,1},{17,9},{25,17},{10,2},{18,10},{26,18},{... | collective-permute-start | bytes 98312 | tf_op jit(solution)/shard_map/ppermute | solution.py:21
  52.8 5.3 %collective-permute-start.3 = (f32[18,1,128]{2,1,0:T(1,128)S(1)}, f32[18,1,128]{2,1,0:T(1,128)S(1)}, u32[]{:S(2)}, u32[]{:S(2)}) collective-permute-start(f32[18,1,128]{2,1,0:T(1,128)S(1)} %get-tuple-element.18), channel_id=1, source_target_pairs={{0,2},{2,4},{4,6},{1,3},{3,5},{5,7},{8,10},{10,12},{12,14},{9,11},... | collective-permute-start | bytes 27656 | tf_op jit(solution)/shard_map/ppermute | solution.py:19
  56.7 5.6 %collective-permute-start.2 = (f32[18,1,128]{2,1,0:T(1,128)S(1)}, f32[18,1,128]{2,1,0:T(1,128)S(1)}, u32[]{:S(2)}, u32[]{:S(2)}) collective-permute-start(f32[18,1,128]{2,1,0:T(1,128)S(1)} %get-tuple-element.19), channel_id=1, source_target_pairs={{2,0},{4,2},{6,4},{3,1},{5,3},{7,5},{10,8},{12,10},{14,12},{11,9},... | collective-permute-start | bytes 27656 | tf_op jit(solution)/shard_map/ppermute | solution.py:21
  62.8 6.3 %collective-permute-start.4 = (f32[18,66,1]{1,2,0:T(1,128)S(1)}, f32[18,66,1]{1,2,0:T(1,128)S(1)}, u32[]{:S(2)}, u32[]{:S(2)}) collective-permute-start(f32[18,66,1]{1,2,0:T(1,128)S(1)} %copy.38), channel_id=1, source_target_pairs={{1,0},{3,2},{5,4},{7,6},{9,8},{11,10},{13,12},{15,14},{17,16},{19,... | collective-permute-start | bytes 14264 | tf_op jit(solution)/shard_map/ppermute | solution.py:21
  64.6 5.9 %collective-permute-start.5 = (f32[18,66,1]{1,2,0:T(1,128)S(1)}, f32[18,66,1]{1,2,0:T(1,128)S(1)}, u32[]{:S(2)}, u32[]{:S(2)}) collective-permute-start(f32[18,66,1]{1,2,0:T(1,128)S(1)} %copy.40), channel_id=1, source_target_pairs={{0,1},{2,3},{4,5},{6,7},{8,9},{10,11},{12,13},{14,15},{16,17},{18,... | collective-permute-start | bytes 14264 | tf_op jit(solution)/shard_map/ppermute | solution.py:19
  115.9 2.6 %collective-permute-start.7 = (f32[1,64,128]{2,1,0:T(8,128)S(1)}, f32[1,64,128]{2,1,0:T(8,128)S(1)}, u32[]{:S(2)}, u32[]{:S(2)}) collective-permute-start(f32[1,64,128]{2,1,0:T(8,128)S(1)} %get-tuple-element.22), channel_id=1, source_target_pairs={{0,8},{8,16},{16,24},{1,9},{9,17},{17,25},{2,10},{10,18},{18,26},{... | collective-permute-start | bytes 98312 | tf_op jit(solution)/shard_map/ppermute | solution.py:19
  117.2 5.9 %collective-permute-start.6 = (f32[1,64,128]{2,1,0:T(8,128)S(1)}, f32[1,64,128]{2,1,0:T(8,128)S(1)}, u32[]{:S(2)}, u32[]{:S(2)}) collective-permute-start(f32[1,64,128]{2,1,0:T(8,128)S(1)} %get-tuple-element.23), channel_id=1, source_target_pairs={{8,0},{16,8},{24,16},{9,1},{17,9},{25,17},{10,2},{18,10},{26,18},{... | collective-permute-start | bytes 98312 | tf_op jit(solution)/shard_map/ppermute | solution.py:21
  123.1 3.5 %collective-permute-start.9 = (f32[18,1,128]{2,1,0:T(1,128)S(1)}, f32[18,1,128]{2,1,0:T(1,128)S(1)}, u32[]{:S(2)}, u32[]{:S(2)}) collective-permute-start(f32[18,1,128]{2,1,0:T(1,128)S(1)} %get-tuple-element.16), channel_id=1, source_target_pairs={{0,2},{2,4},{4,6},{1,3},{3,5},{5,7},{8,10},{10,12},{12,14},{9,11},... | collective-permute-start | bytes 27656 | tf_op jit(solution)/shard_map/ppermute | solution.py:19
  125.3 5.6 %collective-permute-start.8 = (f32[18,1,128]{2,1,0:T(1,128)S(1)}, f32[18,1,128]{2,1,0:T(1,128)S(1)}, u32[]{:S(2)}, u32[]{:S(2)}) collective-permute-start(f32[18,1,128]{2,1,0:T(1,128)S(1)} %get-tuple-element.17), channel_id=1, source_target_pairs={{2,0},{4,2},{6,4},{3,1},{5,3},{7,5},{10,8},{12,10},{14,12},{11,9},... | collective-permute-start | bytes 27656 | tf_op jit(solution)/shard_map/ppermute | solution.py:21
  131.4 6.1 %collective-permute-start.10 = (f32[18,66,1]{1,2,0:T(1,128)S(1)}, f32[18,66,1]{1,2,0:T(1,128)S(1)}, u32[]{:S(2)}, u32[]{:S(2)}) collective-permute-start(f32[18,66,1]{1,2,0:T(1,128)S(1)} %copy.42), channel_id=1, source_target_pairs={{1,0},{3,2},{5,4},{7,6},{9,8},{11,10},{13,12},{15,14},{17,16},{19,... | collective-permute-start | bytes 14264 | tf_op jit(solution)/shard_map/ppermute | solution.py:21
  133.0 5.9 %collective-permute-start.11 = (f32[18,66,1]{1,2,0:T(1,128)S(1)}, f32[18,66,1]{1,2,0:T(1,128)S(1)}, u32[]{:S(2)}, u32[]{:S(2)}) collective-permute-start(f32[18,66,1]{1,2,0:T(1,128)S(1)} %copy.44), channel_id=1, source_target_pairs={{0,1},{2,3},{4,5},{6,7},{8,9},{10,11},{12,13},{14,15},{16,17},{18,... | collective-permute-start | bytes 14264 | tf_op jit(solution)/shard_map/ppermute | solution.py:19
where the time goes:
time: 191 us; the launch traced here: 190 us
  blocking collectives  84.9 us (44%)
  starting transfers between devices  33.5 us (18%)
  waiting for transfers between devices  25.9 us (14%)
  matrix products  18.6 us (10%)
  local copies, waits for them, and re-layouts  11.9 us (6%)
  other arithmetic  8.21 us (4%)
  between operations  7.33 us (4%)
    psum x2, blocking collectives, paired(): lax.psum((jnp.sum(residual * residual), jnp.sum(residual * image)), ('gx'...  84.9 us
    ppermute x6, starting transfers between devices, padded_2(): lax.ppermute(tail, axis, [(i, (i + 1) % count) for i in range(ends)])  17.9 us
    ppermute x6, waiting for transfers between devices, padded_2(): lax.ppermute(head, axis, [((i + 1) % count, i) for i in range(ends)])  15.2 us
    dot_general x1, matrix products, per_device(): tile_sums = jnp.dot(placing, incoming, precision=lax.Precision.HIGHEST)  15.2 us
    ppermute x6, starting transfers between devices, padded_2(): lax.ppermute(head, axis, [((i + 1) % count, i) for i in range(ends)])  7.94 us
    all_to_all x1, waiting for transfers between devices, per_device(): lax.all_to_all(packed.reshape(group_size, CAP, -1), 'gx', split_axis=0, c...  7.51 us
    dot_general x1, local copies, waits for them, and re-layouts, per_device(): tile_sums = jnp.dot(placing, incoming, precision=lax.Precision.HIGHEST)  5.26 us
    all_to_all x1, starting transfers between devices, per_device(): lax.all_to_all(labels, 'gx', split_axis=0, concat_axis=0, tiled=True)  4.26 us
  transfers between devices with their start and end apart: 14, of which 10 were waited for; matrix products, arithmetic and copies ran while one was open for 3% of the time, Pallas kernels for 0%

commit v1 on v0

v1 whole, which is shorter than its diff:
```python
import functools
import math

import jax
import jax.numpy as jnp
from jax import lax
from jax.experimental import pallas as pl
from jax.experimental.pallas import tpu as pltpu
from jax.sharding import PartitionSpec as P

CAP = 2
AXES = ("gx", "gy", "gz")
MESH = pl.DeviceIdType.MESH
F32 = jnp.float32


def offsets_of(sizes, axes):
    found = [()]
    for axis in axes:
        found = [done + (step,) for done in found for step in range(sizes[axis])]
    return [dict(zip(axes, steps)) for steps in found if any(steps)]


def stages_of(sizes):
    stages = []
    for axis in ("gx", "gz", "gy"):
        if sizes[axis] == 1:
            continue
        if stages and math.prod(sizes[a] for a in stages[-1] + [axis]) <= 8:
            stages[-1].append(axis)
        else:
            stages.append([axis])
    return stages


def kernel(
    sizes, stages,
    rank_ref, tile_ref, live_ref, face_hbm, right_hbm, diag_hbm,
    x_ref, r_ref,
    face_v, load_v, diag_v, p_v, q_v, sums_v, send_v, recv_v,
    hx_v, ysend_v, hy_v, zsend_v, hz_v, part_v, gath_v,
    in_sem, a2a_send, a2a_recv, halo_send, halo_recv, red_send, red_recv,
):
    cx, cy, cz = load_v.shape
    blocks = face_v.shape[0]
    group = sizes["gx"]
    at = {axis: lax.axis_index(axis) for axis in AXES}

    def beside(offset):
        return {a: lax.rem(at[a] + s, sizes[a]) for a, s in offset.items() if s}

    loads = [
        pltpu.make_async_copy(face_hbm, face_v, in_sem.at[0]),
        pltpu.make_async_copy(right_hbm, load_v, in_sem.at[1]),
        pltpu.make_async_copy(diag_hbm, diag_v, in_sem.at[2]),
    ]
    for copy in loads:
        copy.start()

    for number, (axis, halo) in enumerate((("gx", hx_v), ("gy", hy_v), ("gz", hz_v))):
        for side in range(2):
            @pl.when(at[axis] == (0 if side == 0 else sizes[axis] - 1))
            def _():
                for turn in range(2):
                    halo[turn, side] = jnp.zeros(halo.shape[2:], F32)

    peers = {}
    for group_axes in [["gx"], ["gy"], ["gz"]] + stages:
        for offset in offsets_of(sizes, group_axes):
            peers[tuple(offset.get(a, 0) for a in AXES)] = offset
    barrier = pltpu.get_barrier_semaphore()
    for offset in peers.values():
        pl.semaphore_signal(barrier, inc=1, device_id=beside(offset), device_id_type=MESH)

    lane = lax.broadcasted_iota(jnp.int32, (cy, cz), 1)
    lane8 = lax.broadcasted_iota(jnp.int32, (8, cz), 1)
    row = lax.broadcasted_iota(jnp.int32, (cy, cz), 0)
    right_half = lane >= cz // 2

    loads[0].wait()
    pair = (
        lax.broadcasted_iota(jnp.int32, (cz, cz), 0) // 2
        == lax.broadcasted_iota(jnp.int32, (cz, cz), 1) % (cz // 2)
    )
    pair = jnp.where(pair, 0.25, 0.0).astype(jnp.bfloat16)
    height = sums_v.shape[0] // cy
    for i in range(cy):
        sums_v[i * height:i * height + blocks, :] = (
            face_v[:, 2 * i * cz:(2 * i + 1) * cz] + face_v[:, (2 * i + 1) * cz:(2 * i + 2) * cz]
        )
        if blocks < height:
            sums_v[i * height + blocks:(i + 1) * height, :] = jnp.zeros((height - blocks, cz), F32)
    whole = sums_v[...]
    high = whole.astype(jnp.bfloat16)
    rest = whole - high.astype(F32)
    middle = rest.astype(jnp.bfloat16)
    low = (rest - middle.astype(F32)).astype(jnp.bfloat16)
    sums_v[...] = (
        jnp.dot(low, pair, preferred_element_type=F32)
        + jnp.dot(middle, pair, preferred_element_type=F32)
    ) + jnp.dot(high, pair, preferred_element_type=F32)

    target = [rank_ref[b] for b in range(blocks)]
    alive = [live_ref[0] > b for b in range(blocks)]
    position = []
    for b in range(blocks):
        count = jnp.int32(0)
        for before in range(b):
            count = count + jnp.where((target[before] == target[b]) & alive[before], 1, 0)
        position.append(count)
    for k in range(group):
        dest = lax.rem(at["gx"] + k, group)
        total = jnp.zeros((cy, cz), F32)
        tags = jnp.full((8, cz), -1.0, F32)
        for b in range(blocks):
            code = jnp.where(alive[b] & (target[b] == dest), position[b], CAP)
            left, right = jnp.where(code == 0, 1.0, 0.0), jnp.where(code == 1, 1.0, 0.0)
            weight = jnp.where(lane8 < cz // 2, left, right)
            tag = tile_ref[b].astype(F32)
            tags = jnp.where(weight > 0.5, tag, tags)
            values = sums_v[pl.ds(b, cy, stride=height), :]
            total = total + values * jnp.where(right_half, right, left)
        (recv_v if k == 0 else send_v)[k, :cy] = total
        (recv_v if k == 0 else send_v)[k, cy:] = tags

    pl.semaphore_wait(barrier, len(peers))
    exchanges = []
    for k in range(1, group):
        copy = pltpu.make_async_remote_copy(
            src_ref=send_v.at[k], dst_ref=recv_v.at[k],
            send_sem=a2a_send.at[k], recv_sem=a2a_recv.at[k],
            device_id=beside({"gx": k}), device_id_type=MESH,
        )
        copy.start()
        exchanges.append(copy)
    loads[1].wait()
    loads[2].wait()
    for copy in exchanges:
        copy.wait_recv()

    want = [(2 * x + jnp.where(lane8 >= cz // 2, 1, 0)).astype(F32)[:1] for x in range(cx)]
    order = [0, cx - 1] + list(range(1, cx - 1))

    def halo_copy(turn, axis, side, src):
        number, halo = AXES.index(axis), (hx_v, hy_v, hz_v)[AXES.index(axis)]
        step = sizes[axis] - 1 if side == 0 else 1
        return pltpu.make_async_remote_copy(
            src_ref=src, dst_ref=halo.at[turn, 1 - side],
            send_sem=halo_send.at[turn, 2 * number + side],
            recv_sem=halo_recv.at[turn, 2 * number + 1 - side],
            device_id={axis: lax.rem(at[axis] + step, sizes[axis])}, device_id_type=MESH,
        )

    def faces(turn, field, axis):
        if axis == "gx":
            return field.at[0], field.at[cx - 1]
        if axis == "gy":
            return ysend_v.at[turn, 0], ysend_v.at[turn, 1]
        return zsend_v.at[turn], zsend_v.at[turn]

    def near(axis, side):
        return at[axis] > 0 if side == 0 else at[axis] < sizes[axis] - 1

    def send(turn, field, axis):
        for side in range(2):
            @pl.when(near(axis, side))
            def _():
                halo_copy(turn, axis, side, faces(turn, field, axis)[side]).start()

    def receive(turn, field, axis):
        for side in range(2):
            @pl.when(near(axis, side))
            def _():
                halo_copy(turn, axis, 1 - side, faces(turn, field, axis)[1 - side]).wait_recv()

    def finish(turn, field, axis):
        for side in range(2):
            @pl.when(near(axis, side))
            def _():
                halo_copy(turn, axis, side, faces(turn, field, axis)[side]).wait_send()

    def pack(turn, x, plane, packed):
        ysend_v[turn, 0, x:x + 1] = plane[:1]
        ysend_v[turn, 1, x:x + 1] = plane[cy - 1:]
        turned = plane if x == 0 else pltpu.roll(plane, 2 * x, axis=1)
        return jnp.where(((lane + 1) % cz) // 2 == x, turned, packed)

    packed = jnp.zeros((cy, cz), F32)
    for x in order:
        plane = load_v[x]
        for k in range(group):
            values, tags = recv_v[k, :cy], recv_v[k, cy:cy + 1]
            plane = plane + jnp.where(tags == want[x], values, 0.0)
            plane = plane + jnp.where(
                pltpu.roll(recv_v[k, cy:], cz // 2, axis=1)[:1] == want[x],
                pltpu.roll(values, cz // 2, axis=1), 0.0,
            )
        load_v[x] = plane
        packed = pack(0, x, plane, packed)
        if x == cx - 1:
            send(0, load_v, "gx")
    zsend_v[0] = packed
    send(0, load_v, "gz")
    send(0, load_v, "gy")

    def inside(src, dst):
        for x in range(cx):
            plane = src[x]
            around = jnp.where(lane == 0, 0.0, pltpu.roll(plane, 1, axis=1))
            around = around + jnp.where(lane == cz - 1, 0.0, pltpu.roll(plane, cz - 1, axis=1))
            around = around + jnp.where(row == 0, 0.0, pltpu.roll(plane, 1, axis=0))
            around = around + jnp.where(row == cy - 1, 0.0, pltpu.roll(plane, cy - 1, axis=0))
            if x > 0:
                around = around + src[x - 1]
            if x < cx - 1:
                around = around + src[x + 1]
            dst[x] = diag_v[x] * plane - around

    def fold(acc, values):
        for part in range(cy // 8):
            acc = acc + values[8 * part:8 * part + 8]
        return acc

    def border(turn, src, dst, sink):
        for axis in ("gx", "gz", "gy"):
            receive(turn, src, axis)
        ahead, behind = hz_v[turn, 1], pltpu.roll(hz_v[turn, 0], 2, axis=1)
        merged = jnp.where(lane % 2 == 0, ahead, behind)
        for x in order:
            edge = pltpu.roll(merged, cz - 2 * x - 1, axis=1)
            plane = dst[x] - jnp.where((lane == 0) | (lane == cz - 1), edge, 0.0)
            plane = plane - jnp.where(row == 0, hy_v[turn, 0, x:x + 1], 0.0)
            plane = plane - jnp.where(row == cy - 1, hy_v[turn, 1, x:x + 1], 0.0)
            if x == 0:
                plane = plane - hx_v[turn, 0]
            if x == cx - 1:
                plane = plane - hx_v[turn, 1]
            dst[x] = plane
            sink(x, plane)

    inside(load_v, p_v)
    state = {"packed": jnp.zeros((cy, cz), F32)}

    def first(x, plane):
        state["packed"] = pack(1, x, plane, state["packed"])
        if x == cx - 1:
            send(1, p_v, "gx")

    border(0, load_v, p_v, first)
    zsend_v[1] = state["packed"]
    send(1, p_v, "gz")
    send(1, p_v, "gy")
    inside(p_v, q_v)
    acc = [jnp.zeros((8, cz), F32) for _ in range(4)]
    for x in range(cx):
        load, p = load_v[x], p_v[x]
        acc[0], acc[1], acc[2] = fold(acc[0], load * load), fold(acc[1], load * p), fold(acc[2], p * p)

    def second(x, plane):
        acc[3] = fold(acc[3], plane * p_v[x])

    border(1, p_v, q_v, second)

    row8 = lax.broadcasted_iota(jnp.int32, (8, cz), 0)
    mine = jnp.zeros((8, cz), F32)
    for number in range(4):
        mine = jnp.where(row8 == number, jnp.sum(acc[number], axis=0, keepdims=True), mine)
    slot = 0
    waiting = []
    for number, axes in enumerate(stages):
        part_v[number] = mine
        copies = []
        for offset in offsets_of(sizes, axes):
            copy = pltpu.make_async_remote_copy(
                src_ref=part_v.at[number], dst_ref=gath_v.at[slot],
                send_sem=red_send.at[slot], recv_sem=red_recv.at[slot],
                device_id=beside(offset), device_id_type=MESH,
            )
            copy.start()
            copies.append((slot, copy))
            slot += 1
        for at_slot, copy in copies:
            copy.wait_recv()
            mine = mine + gath_v[at_slot]
        waiting += [copy for _, copy in copies]

    sums = jnp.sum(mine, axis=1, keepdims=True)
    s0, s1, s2, s3 = (sums[n:n + 1] for n in range(4))
    step = 6.0 * s0 + s1
    a = s0 / step
    c = s1 / step
    norm = c * c * s0 - 2.0 * a * c * s1 + a * a * s2
    e = c + norm / s0
    curve = 6.0 * (e * e * s0 - 2.0 * e * a * s1 + a * a * s2) + (
        e * e * s1 - 2.0 * e * a * s2 + a * a * s3
    )
    b = norm / curve
    x_load, x_p = a + b * e, b * a
    r_load, r_p, r_q = c - 6.0 * b * e, a + b * (e - 6.0 * a), b * a
    for x in range(cx):
        load, p = load_v[x], p_v[x]
        x_ref[x] = x_load * load - x_p * p
        r_ref[x] = r_load * load - r_p * p + r_q * q_v[x]

    for copy in exchanges + waiting:
        copy.wait_send()
    for turn, field in ((0, load_v), (1, p_v)):
        for axis in AXES:
            finish(turn, field, axis)


def per_device(sizes, face_blocks, owner_rank, owner_tile, live_count, right_side, diagonal):
    blocks, width = face_blocks.shape[3:]
    cx, cy, cz = right_side.shape
    height = -(-blocks // 8) * 8
    group = sizes["gx"]
    stages = stages_of(sizes)
    slots = sum(len(offsets_of(sizes, axes)) for axes in stages)
    smem, vmem, anywhere = (
        pl.BlockSpec(memory_space=space) for space in (pltpu.SMEM, pltpu.VMEM, pl.ANY)
    )
    box = jax.ShapeDtypeStruct((cx, cy, cz), F32)
    return pl.pallas_call(
        functools.partial(kernel, sizes, stages),
        out_shape=(box, box),
        in_specs=[smem] * 3 + [anywhere] * 3,
        out_specs=(vmem, vmem),
        scratch_shapes=[
            pltpu.VMEM((blocks, width), F32),
            pltpu.VMEM((cx, cy, cz), F32),
            pltpu.VMEM((cx, cy, cz), F32),
            pltpu.VMEM((cx, cy, cz), F32),
            pltpu.VMEM((cx, cy, cz), F32),
            pltpu.VMEM((cy * height, cz), F32),
            pltpu.VMEM((group, cy + 8, cz), F32),
            pltpu.VMEM((group, cy + 8, cz), F32),
            pltpu.VMEM((2, 2, cy, cz), F32),
            pltpu.VMEM((2, 2, cx, cz), F32),
            pltpu.VMEM((2, 2, cx, cz), F32),
            pltpu.VMEM((2, cy, cz), F32),
            pltpu.VMEM((2, 2, cy, cz), F32),
            pltpu.VMEM((len(stages), 8, cz), F32),
            pltpu.VMEM((slots, 8, cz), F32),
            pltpu.SemaphoreType.DMA((3,)),
            pltpu.SemaphoreType.DMA((group,)),
            pltpu.SemaphoreType.DMA((group,)),
            pltpu.SemaphoreType.DMA((2, 6)),
            pltpu.SemaphoreType.DMA((2, 6)),
            pltpu.SemaphoreType.DMA((slots,)),
            pltpu.SemaphoreType.DMA((slots,)),
        ],
        compiler_params=pltpu.CompilerParams(collective_id=0, has_side_effects=True),
    )(
        owner_rank.reshape(blocks), owner_tile.reshape(blocks), live_count.reshape(1),
        face_blocks.reshape(blocks, width), right_side, diagonal,
    )


def solution(mesh):
    sizes = dict(mesh.shape)
    return jax.shard_map(
        functools.partial(per_device, sizes),
        mesh=mesh,
        in_specs=(
            P("gx", "gy", "gz", None, None),
            P("gx", "gy", "gz", None, None),
            P("gx", "gy", "gz", None),
            P("gx", "gy", "gz"),
            P("gx", "gy", "gz"),
            P("gx", "gy", "gz"),
        ),
        out_specs=(P("gx", "gy", "gz"), P("gx", "gy", "gz")),
        check_vma=False,
    )
```

time: 191 us -> 32.4 us (0.17)
  blocking collectives: 84.9 us -> 0 us
  starting transfers between devices: 33.5 us -> 0 us
  Pallas kernels: 0 us -> 26.2 us
  waiting for transfers between devices: 25.9 us -> 0 us
  matrix products: 18.6 us -> 0 us
  other arithmetic: 8.21 us -> 0 us
  local copies, waits for them, and re-layouts: 11.9 us -> 4.77 us
  between operations: 7.33 us -> 1.29 us
    psum x2 -> x0, blocking collectives: 84.9 us -> none  [paired(): lax.psum((jnp.sum(residual * residual), jnp.sum(residual * image)), ('gx'...]
    pallas_call x0 -> x1, Pallas kernels: none -> 26.2 us  [per_device(): pl.pallas_call(functools.partial(kernel, sizes, stages), out_shape=(box,...]
    ppermute x12 -> x0, starting transfers between devices: 25.8 us -> none  [the longest x6 17.9 us: padded_2(): lax.ppermute(tail, axis, [(i, (i + 1) % count) for i in range(ends)])]
    dot_general x3 -> x0, matrix products: 18.6 us -> none  [the longest x1 15.2 us: per_device(): tile_sums = jnp.dot(placing, incoming, precision=lax.Precision.HIGHEST)]
    ppermute x12 -> x0, waiting for transfers between devices: 17.3 us -> none  [the longest x6 15.2 us: padded_2(): lax.ppermute(head, axis, [((i + 1) % count, i) for i in range(ends)])]
    all_to_all x2 -> x0, waiting for transfers between devices: 8.53 us -> none  [the longest x1 7.51 us: per_device(): lax.all_to_all(packed.reshape(group_size, CAP, -1), 'gx', split_axis=0, c...]
    all_to_all x2 -> x0, starting transfers between devices: 7.74 us -> none  [the longest x1 4.26 us: per_device(): lax.all_to_all(labels, 'gx', split_axis=0, concat_axis=0, tiled=True)]
    dot_general x1 -> x0, local copies, waits for them, and re-layouts: 5.26 us -> none  [per_device(): tile_sums = jnp.dot(placing, incoming, precision=lax.Precision.HIGHEST)]
  transfers between devices with their start and end apart: 14 -> 0, of which waited for: 10 -> 0; matrix products, arithmetic and copies ran while one was open for 3% -> 0% of each run, Pallas kernels for 0% -> 0%
where the time goes in v1:
time: 32.4 us; the launch traced here: 32.2 us
  Pallas kernels  26.2 us (81%)
  local copies, waits for them, and re-layouts  4.77 us (15%)
  between operations  1.29 us (4%)
    pallas_call x1, Pallas kernels, per_device(): pl.pallas_call(functools.partial(kernel, sizes, stages), out_shape=(box,...  26.2 us
    unnamed x5, local copies, waits for them, and re-layouts  4.77 us

profile of v1, /device:TPU:0, one launch (start us, length us, event | category | flops | bytes accessed | tf_op | source)
XLA Modules:
  0.0 32.2 jit_solution(8975417101937427196)
XLA Ops:
  1.3 2.0 %copy.10 = f32[1,1,1,6,16384]{4,3,2,1,0:T(8,128)} copy(f32[1,1,1,6,16384]{4,2,3,1,0:T(1,128)} %param.6) | data formatting | bytes 786432
  3.3 26.2 %shard_map.77 = (f32[16,64,128]{2,1,0:T(8,128)}, f32[16,64,128]{2,1,0:T(8,128)}) custom-call(s32[6]{0:T(128)} %bitcast.8, s32[6]{0:T(128)} %bitcast.9, s32[1]{0:T(128)} %bitcast.6.live_ref, f32[6,16384]{1,0:T(8,128)} %bitcast.7, f32[16,64,128]{2,1,0:T(8,128)} %right_hbm.1, f32[16,64,128]{2,1,0:T(8,128)} %diag_hbm.1), custom_call_target="tpu_custom_call" | custom-call | tf_op jit(solution)/shard_map/pallas_call | solution.py:323
  29.5 0.0 copy-start
  29.5 1.9 %copy.14 = f32[16,64,128]{2,1,0:T(8,128)} copy(f32[16,64,128]{2,1,0:T(8,128)} %get-tuple-element.4) | data formatting | bytes 1048576
  31.4 0.0 copy-done
  31.4 0.8 %copy.15 = f32[16,64,128]{2,1,0:T(8,128)} copy(f32[16,64,128]{2,1,0:T(8,128)S(1)} %copy-done) | data formatting | bytes 1048576
Async XLA Ops:
  29.5 2.0 %copy-start = (f32[16,64,128]{2,1,0:T(8,128)S(1)}, f32[16,64,128]{2,1,0:T(8,128)}, u32[]{:S(2)}) copy-start(f32[16,64,128]{2,1,0:T(8,128)} %get-tuple-element.5) | copy-start | bytes 1572868

commit v2 on v1

--- a/solution.py
+++ b/solution.py
@@ -24,8 +24,6 @@
 def stages_of(sizes):
     stages = []
     for axis in ("gx", "gz", "gy"):
-        if sizes[axis] == 1:
-            continue
         if stages and math.prod(sizes[a] for a in stages[-1] + [axis]) <= 8:
             stages[-1].append(axis)
         else:
@@ -35,17 +33,20 @@
 
 def kernel(
     sizes, stages,
-    rank_ref, tile_ref, live_ref, face_hbm, right_hbm, diag_hbm,
-    x_ref, r_ref,
-    face_v, load_v, diag_v, p_v, q_v, sums_v, send_v, recv_v,
+    rank_ref, tile_ref, live_hbm, face_hbm, right_hbm, diag_hbm,
+    load_hbm, p_hbm, q_hbm, coef_ref,
+    live_ref, face_v, load_v, diag_v, p_v, q_v, sums_v, send_v, recv_v, turned_v,
     hx_v, ysend_v, hy_v, zsend_v, hz_v, part_v, gath_v,
-    in_sem, a2a_send, a2a_recv, halo_send, halo_recv, red_send, red_recv,
+    in_sem, out_sem, a2a_send, a2a_recv, halo_send, halo_recv, red_send, red_recv,
 ):
     cx, cy, cz = load_v.shape
     blocks = face_v.shape[0]
     group = sizes["gx"]
     at = {axis: lax.axis_index(axis) for axis in AXES}
 
+    def near(axis, side):
+        return at[axis] > 0 if side == 0 else at[axis] < sizes[axis] - 1
+
     def beside(offset):
         return {a: lax.rem(at[a] + s, sizes[a]) for a, s in offset.items() if s}
 
@@ -53,6 +54,7 @@
         pltpu.make_async_copy(face_hbm, face_v, in_sem.at[0]),
         pltpu.make_async_copy(right_hbm, load_v, in_sem.at[1]),
         pltpu.make_async_copy(diag_hbm, diag_v, in_sem.at[2]),
+        pltpu.make_async_copy(live_hbm, live_ref, in_sem.at[3]),
     ]
     for copy in loads:
         copy.start()
@@ -78,18 +80,16 @@
     right_half = lane >= cz // 2
 
     loads[0].wait()
+    loads[3].wait()
     pair = (
         lax.broadcasted_iota(jnp.int32, (cz, cz), 0) // 2
         == lax.broadcasted_iota(jnp.int32, (cz, cz), 1) % (cz // 2)
     )
     pair = jnp.where(pair, 0.25, 0.0).astype(jnp.bfloat16)
-    height = sums_v.shape[0] // cy
-    for i in range(cy):
-        sums_v[i * height:i * height + blocks, :] = (
-            face_v[:, 2 * i * cz:(2 * i + 1) * cz] + face_v[:, (2 * i + 1) * cz:(2 * i + 2) * cz]
+    for b in range(blocks):
+        sums_v[b * cy:(b + 1) * cy] = (
+            face_v[b, pl.ds(0, cy, stride=2), :] + face_v[b, pl.ds(1, cy, stride=2), :]
         )
-        if blocks < height:
-            sums_v[i * height + blocks:(i + 1) * height, :] = jnp.zeros((height - blocks, cz), F32)
     whole = sums_v[...]
     high = whole.astype(jnp.bfloat16)
     rest = whole - high.astype(F32)
@@ -101,7 +101,7 @@
     ) + jnp.dot(high, pair, preferred_element_type=F32)
 
     target = [rank_ref[b] for b in range(blocks)]
-    alive = [live_ref[0] > b for b in range(blocks)]
+    alive = [live_ref[0, 0, 0] > b for b in range(blocks)]
     position = []
     for b in range(blocks):
         count = jnp.int32(0)
@@ -118,7 +118,7 @@
             weight = jnp.where(lane8 < cz // 2, left, right)
             tag = tile_ref[b].astype(F32)
             tags = jnp.where(weight > 0.5, tag, tags)
-            values = sums_v[pl.ds(b, cy, stride=height), :]
+            values = sums_v[b * cy:(b + 1) * cy]
             total = total + values * jnp.where(right_half, right, left)
         (recv_v if k == 0 else send_v)[k, :cy] = total
         (recv_v if k == 0 else send_v)[k, cy:] = tags
@@ -138,6 +138,8 @@
     for copy in exchanges:
         copy.wait_recv()
 
+    for k in range(group):
+        turned_v[k] = pltpu.roll(recv_v[k], cz // 2, axis=1)
     want = [(2 * x + jnp.where(lane8 >= cz // 2, 1, 0)).astype(F32)[:1] for x in range(cx)]
     order = [0, cx - 1] + list(range(1, cx - 1))
 
@@ -158,9 +160,6 @@
             return ysend_v.at[turn, 0], ysend_v.at[turn, 1]
         return zsend_v.at[turn], zsend_v.at[turn]
 
-    def near(axis, side):
-        return at[axis] > 0 if side == 0 else at[axis] < sizes[axis] - 1
-
     def send(turn, field, axis):
         for side in range(2):
             @pl.when(near(axis, side))
@@ -192,8 +191,7 @@
             values, tags = recv_v[k, :cy], recv_v[k, cy:cy + 1]
             plane = plane + jnp.where(tags == want[x], values, 0.0)
             plane = plane + jnp.where(
-                pltpu.roll(recv_v[k, cy:], cz // 2, axis=1)[:1] == want[x],
-                pltpu.roll(values, cz // 2, axis=1), 0.0,
+                turned_v[k, cy:cy + 1] == want[x], turned_v[k, :cy], 0.0
             )
         load_v[x] = plane
         packed = pack(0, x, plane, packed)
@@ -202,6 +200,13 @@
     zsend_v[0] = packed
     send(0, load_v, "gz")
     send(0, load_v, "gy")
+
+    stores = [
+        pltpu.make_async_copy(load_v, load_hbm, out_sem.at[0]),
+        pltpu.make_async_copy(p_v, p_hbm, out_sem.at[1]),
+        pltpu.make_async_copy(q_v, q_hbm, out_sem.at[2]),
+    ]
+    stores[0].start()
 
     def inside(src, dst):
         for x in range(cx):
@@ -250,6 +255,7 @@
     zsend_v[1] = state["packed"]
     send(1, p_v, "gz")
     send(1, p_v, "gy")
+    stores[1].start()
     inside(p_v, q_v)
     acc = [jnp.zeros((8, cz), F32) for _ in range(4)]
     for x in range(cx):
@@ -260,6 +266,7 @@
         acc[3] = fold(acc[3], plane * p_v[x])
 
     border(1, p_v, q_v, second)
+    stores[2].start()
 
     row8 = lax.broadcasted_iota(jnp.int32, (8, cz), 0)
     mine = jnp.zeros((8, cz), F32)
@@ -297,11 +304,10 @@
     b = norm / curve
     x_load, x_p = a + b * e, b * a
     r_load, r_p, r_q = c - 6.0 * b * e, a + b * (e - 6.0 * a), b * a
-    for x in range(cx):
-        load, p = load_v[x], p_v[x]
-        x_ref[x] = x_load * load - x_p * p
-        r_ref[x] = r_load * load - r_p * p + r_q * q_v[x]
-
+    for number, value in enumerate((x_load, x_p, r_load, r_p, r_q)):
+        coef_ref[number:number + 1] = jnp.broadcast_to(value, (1, cz))
+    for copy in stores:
+        copy.wait()
     for copy in exchanges + waiting:
         copy.wait_send()
     for turn, field in ((0, load_v), (1, p_v)):
@@ -309,10 +315,31 @@
             finish(turn, field, axis)
 
 
+def combine(load_ref, p_ref, q_ref, coef_ref, x_ref, r_ref):
+    x_load, x_p, r_load, r_p, r_q = (coef_ref[n:n + 1] for n in range(5))
+    for x in range(load_ref.shape[0]):
+        load, p = load_ref[x], p_ref[x]
+        x_ref[x] = x_load * load - x_p * p
+        r_ref[x] = r_load * load - r_p * p + r_q * q_ref[x]
+
+
+def combined(load, p, q, coef):
+    cx, cy, cz = load.shape
+    parts = 2 if cx % 2 == 0 else 1
+    piece = pl.BlockSpec((cx // parts, cy, cz), lambda i: (i, 0, 0))
+    box = jax.ShapeDtypeStruct((cx, cy, cz), F32)
+    return pl.pallas_call(
+        combine,
+        grid=(parts,),
+        out_shape=(box, box),
+        in_specs=[piece] * 3 + [pl.BlockSpec((8, cz), lambda i: (0, 0))],
+        out_specs=(piece, piece),
+    )(load, p, q, coef)
+
+
 def per_device(sizes, face_blocks, owner_rank, owner_tile, live_count, right_side, diagonal):
-    blocks, width = face_blocks.shape[3:]
+    blocks = face_blocks.shape[3]
     cx, cy, cz = right_side.shape
-    height = -(-blocks // 8) * 8
     group = sizes["gx"]
     stages = stages_of(sizes)
     slots = sum(len(offsets_of(sizes, axes)) for axes in stages)
@@ -320,18 +347,20 @@
         pl.BlockSpec(memory_space=space) for space in (pltpu.SMEM, pltpu.VMEM, pl.ANY)
     )
     box = jax.ShapeDtypeStruct((cx, cy, cz), F32)
-    return pl.pallas_call(
+    load, p, q, coef = pl.pallas_call(
         functools.partial(kernel, sizes, stages),
-        out_shape=(box, box),
-        in_specs=[smem] * 3 + [anywhere] * 3,
-        out_specs=(vmem, vmem),
+        out_shape=(box, box, box, jax.ShapeDtypeStruct((8, cz), F32)),
+        in_specs=[smem] * 2 + [anywhere] * 4,
+        out_specs=(anywhere, anywhere, anywhere, vmem),
         scratch_shapes=[
-            pltpu.VMEM((blocks, width), F32),
+            pltpu.SMEM(live_count.shape, jnp.int32),
+            pltpu.VMEM((blocks, 2 * cy, cz), F32),
             pltpu.VMEM((cx, cy, cz), F32),
             pltpu.VMEM((cx, cy, cz), F32),
             pltpu.VMEM((cx, cy, cz), F32),
             pltpu.VMEM((cx, cy, cz), F32),
-            pltpu.VMEM((cy * height, cz), F32),
+            pltpu.VMEM((blocks * cy, cz), F32),
+            pltpu.VMEM((group, cy + 8, cz), F32),
             pltpu.VMEM((group, cy + 8, cz), F32),
             pltpu.VMEM((group, cy + 8, cz), F32),
             pltpu.VMEM((2, 2, cy, cz), F32),
@@ -341,6 +370,7 @@
             pltpu.VMEM((2, 2, cy, cz), F32),
             pltpu.VMEM((len(stages), 8, cz), F32),
             pltpu.VMEM((slots, 8, cz), F32),
+            pltpu.SemaphoreType.DMA((4,)),
             pltpu.SemaphoreType.DMA((3,)),
             pltpu.SemaphoreType.DMA((group,)),
             pltpu.SemaphoreType.DMA((group,)),
@@ -351,9 +381,10 @@
         ],
         compiler_params=pltpu.CompilerParams(collective_id=0, has_side_effects=True),
     )(
-        owner_rank.reshape(blocks), owner_tile.reshape(blocks), live_count.reshape(1),
-        face_blocks.reshape(blocks, width), right_side, diagonal,
+        owner_rank.reshape(blocks), owner_tile.reshape(blocks), live_count,
+        face_blocks.reshape(blocks, 2 * cy, cz), right_side, diagonal,
     )
+    return combined(load, p, q, coef)
 
 
 def solution(mesh):

time: 32.4 us -> 28.3 us (0.87)
  local copies, waits for them, and re-layouts: 4.77 us -> 0 us
  Pallas kernels: 26.2 us -> 26.8 us
    unnamed x5 -> x0, local copies, waits for them, and re-layouts: 4.77 us -> none
    pallas_call x0 -> x1, Pallas kernels: none -> 2.23 us  [combined(): pl.pallas_call(combine, grid=(parts,), out_shape=(box, box), in_specs=[pi...]
    pallas_call x1, Pallas kernels: 26.2 us -> 24.6 us  [per_device(): pl.pallas_call(functools.partial(kernel, sizes, stages), out_shape=(box,...]
where the time goes in v2:
time: 28.3 us; the launch traced here: 28.1 us
  Pallas kernels  26.8 us (95%)
  between operations  1.28 us (5%)
    pallas_call x1, Pallas kernels, per_device(): pl.pallas_call(functools.partial(kernel, sizes, stages), out_shape=(box,...  24.6 us
    pallas_call x1, Pallas kernels, combined(): pl.pallas_call(combine, grid=(parts,), out_shape=(box, box), in_specs=[pi...  2.23 us

profile of v2, /device:TPU:0, one launch (start us, length us, event | category | flops | bytes accessed | tf_op | source)
XLA Modules:
  0.0 28.1 jit_solution(857470893454359921)
XLA Ops:
  1.3 24.6 %shard_map.77 = (f32[16,64,128]{2,1,0:T(8,128)}, f32[16,64,128]{2,1,0:T(8,128)}, f32[16,64,128]{2,1,0:T(8,128)}, f32[8,128]{1,0:T(8,128)}) custom-call(s32[6]{0:T(128)} %bitcast.4, s32[6]{0:T(128)} %bitcast.5, s32[1,1,1]{2,1,0:T(1,128)S(6)} %copy.8.live_hbm, f32[6,128,128]{2,1,0:T(8,128)} %bitcast.3, f32[16,64,128]{2,1,0:T(8,128)} %right_hbm.1, ...), custom_call_target="tpu_custom_call" | custom-call | tf_op jit(solution)/shard_map/pallas_call | solution.py:350
  25.9 2.2 %shard_map.78 = (f32[16,64,128]{2,1,0:T(8,128)}, f32[16,64,128]{2,1,0:T(8,128)}) custom-call(f32[16,64,128]{2,1,0:T(8,128)} %get-tuple-element.6.load_ref, f32[16,64,128]{2,1,0:T(8,128)} %get-tuple-element.7.p_ref, f32[16,64,128]{2,1,0:T(8,128)} %get-tuple-element.8.q_ref, f32[8,128]{1,0:T(8,128)} %get-tuple-element.9.coef_ref), custom_call_target="tpu_custom_call" | custom-call | tf_op jit(solution)/shard_map/pallas_call | solution.py:331
